TPU v7x, 32 devices: a whole 2x2x4 slice. The times are simulated.
32 devices in a mesh: row: 2 (over x), col: 16 (over z, y, core).
Axes of the slice: x: 2, y: 2, z: 4, core: 2. Of those that a mesh axis runs over, the one named last changes fastest.
Arguments:
- rhs_fields: float32 [4, 256, 4096], P(None, 'row', 'col'), may hold values from -6 to 6
- coupling: float32 [256, 4096], P('row', 'col'), may hold values from 1 to 8
- inv_pivot: float32 [2, 1024, 1024], P('row', 'col'), may hold values from -0.75 to 0.75
- lower_factor: float32 [2, 1024, 1024], P('row', 'col'), may hold values from -0.125 to 0.125
- upper_factor: float32 [2, 1024, 1024], P('row', 'col'), may hold values from -0.125 to 0.125
Outputs:
- correction: float32 [4, 256, 4096], P(None, 'row', 'col')
All inputs are finite; a program needn't handle non-finite values.
Results may differ from a plain program's by a relative error of at most 0.0001.
Values sent between devices are 32-bit elements; how exact they have to be, the bound alone decides.
No kernel may reach another device: no remote copies, remote signals or barrier semaphores. Data moves between devices by JAX's collectives and lax.ppermute only.
A program may use at most 64 MiB of HBM per device.

v0:
```python
import jax
import jax.numpy as jnp
from jax import lax
from jax.sharding import PartitionSpec as P

SWEEPS = 4
SUB = 8


def extended(block, sides, width):
    for axis, dim in sides:
        count = lax.axis_size(axis)
        forward = [(i, i + 1) for i in range(count - 1)]
        backward = [(target, source) for source, target in forward]
        low = lax.ppermute(
            lax.slice_in_dim(block, block.shape[dim] - width, None, axis=dim), axis, forward
        )
        high = lax.ppermute(lax.slice_in_dim(block, 0, width, axis=dim), axis, backward)
        block = jnp.concatenate([low, block, high], axis=dim)
    return block


def from_behind(value, axis, steps):
    count = lax.axis_size(axis)
    first, last = (max(0, -steps), min(count, count - steps))
    return lax.ppermute(value, axis, [(source, source + steps) for source in range(first, last)])


def face_terms(padded):
    center = padded[1:-1, 1:-1]
    upward = 0.5 * (center + padded[:-2, 1:-1])
    downward = 0.5 * (center + padded[2:, 1:-1])
    leftward = 0.5 * (center + padded[1:-1, :-2])
    rightward = 0.5 * (center + padded[1:-1, 2:])
    diagonal = 1.0 + upward + downward + leftward + rightward
    return (upward, downward, leftward, rightward, diagonal)


def relax_once(padded, source, terms):
    upward, downward, leftward, rightward, diagonal = terms
    total = source + upward * padded[:, :-2, 1:-1]
    total = total + downward * padded[:, 2:, 1:-1]
    total = total + leftward * padded[:, 1:-1, :-2]
    total = total + rightward * padded[:, 1:-1, 2:]
    return total / diagonal


def hdot(left, right):
    return jnp.dot(left, right, precision=lax.Precision.HIGHEST)


def crop_region(array, offset, extent_x, extent_y):
    return array[..., offset : offset + extent_x, offset : offset + extent_y]


def on_device(rhs_fields, coupling, inv_pivot, lower_factor, upper_factor):
    count, extent_x, extent_y = rhs_fields.shape
    stacked = jnp.concatenate([rhs_fields, coupling[None]], axis=0)
    widened = extended(stacked, (("row", 1), ("col", 2)), SWEEPS)
    source = widened[:-1]
    terms_full = face_terms(widened[-1])
    total_x = extent_x * lax.axis_size("row")
    total_y = extent_y * lax.axis_size("col")
    global_x = (
        lax.axis_index("row") * extent_x
        - SWEEPS
        + jnp.arange(extent_x + 2 * SWEEPS, dtype=jnp.int32)
    )
    global_y = (
        lax.axis_index("col") * extent_y
        - SWEEPS
        + jnp.arange(extent_y + 2 * SWEEPS, dtype=jnp.int32)
    )
    inside_x = jnp.logical_and(global_x >= 0, global_x < total_x)
    inside_y = jnp.logical_and(global_y >= 0, global_y < total_y)
    inside = jnp.logical_and(inside_x[:, None], inside_y[None, :]).astype(jnp.float32)
    fine = source
    for repeat in range(SWEEPS):
        margin = SWEEPS - 1 - repeat
        size_x = extent_x + 2 * margin
        size_y = extent_y + 2 * margin
        terms = tuple((crop_region(term, repeat, size_x, size_y) for term in terms_full))
        fine = relax_once(fine, crop_region(source, repeat + 1, size_x, size_y), terms)
        fine = fine * crop_region(inside, repeat + 1, size_x, size_y)
    row_index = lax.axis_index("row")
    rows = lax.axis_size("row")
    pivot = inv_pivot[0]
    lower = lower_factor[0]
    upper = upper_factor[0]
    own_count = pivot.shape[0]
    block_count = pivot.shape[1]
    sub_x = extent_x // SUB
    sub_y = extent_y // SUB
    coarse = (
        rhs_fields.reshape(count, SUB, sub_x, SUB, sub_y)
        .mean(axis=(2, 4))
        .reshape(count, own_count)
    )
    coarse_full = lax.all_gather(coarse, "col", axis=1, tiled=True)
    driven = hdot(coarse_full, pivot.T)

    def forward_turn(turn, carry):
        incoming, stored = carry
        update = driven - hdot(incoming, lower.T)
        stored = jnp.where(row_index == turn, update, stored)
        gathered = lax.all_gather(stored, "col", axis=1, tiled=True)
        incoming = from_behind(gathered, "row", 1)
        return (incoming, stored)

    start = (
        jnp.zeros((count, block_count), jnp.float32),
        jnp.zeros((count, own_count), jnp.float32),
    )
    unused, downs = lax.fori_loop(0, rows, forward_turn, start)

    def backward_turn(turn, carry):
        incoming, stored = carry
        update = downs - hdot(incoming, upper.T)
        stored = jnp.where(row_index == rows - 1 - turn, update, stored)
        gathered = lax.all_gather(stored, "col", axis=1, tiled=True)
        incoming = from_behind(gathered, "row", -1)
        return (incoming, stored)

    unused, solved = lax.fori_loop(0, rows, backward_turn, start)
    result = fine.reshape(count, SUB, sub_x, SUB, sub_y) + solved.reshape(count, SUB, 1, SUB, 1)
    return result.reshape(count, extent_x, extent_y)


def solution(mesh):
    return jax.shard_map(
        on_device,
        mesh=mesh,
        in_specs=(
            P(None, "row", "col"),
            P("row", "col"),
            P("row", "col", None),
            P("row", "col", None),
            P("row", "col", None),
        ),
        out_specs=P(None, "row", "col"),
        check_vma=False,
    )
```

profile of v0, /device:TPU:5, one launch (start us, length us, event | category | flops | bytes accessed | tf_op | source)
XLA Modules:
  0.0 144.4 jit_solution(1100728460635912829)
XLA Ops:
  0.9 3.1 %collective-permute-start.2 = (f32[5,4,256]{2,1,0:T(4,128)S(1)}, f32[5,4,256]{2,1,0:T(4,128)S(1)}, u32[]{:S(2)}, u32[]{:S(2)}) collective-permute-start(f32[5,4,256]{2,1,0:T(4,128)S(1)} %get-tuple-element.298), channel_id=1, source_target_pairs={{0,16},{1,17},{2,18},{3,19},{4,20},{5,21},{6,22},{7,23},{8,24},{9,... | collective-permute-start | bytes 61448 | tf_op jit(solution)/shard_map/ppermute | solution.py:15
  4.0 1.3 collective-permute-start.3
  5.3 1.6 %reshape.50 = f32[4,8,16,8,32]{4,3,2,1,0:T(8,128)S(1)} reshape(f32[4,128,256]{2,1,0:T(8,128)} %param.9) | data formatting | bytes 1048576 | tf_op jit(solution)/shard_map/reshape | solution.py:95
  7.3 18.8 %all-gather.2 = f32[16,64,4]{1,2,0:T(4,128)S(1)} all-gather(f32[1,64,4]{1,2,0:T(4,128)S(1)} %bitcast.57), channel_id=1, replica_groups=mesh['row'=2,'col'=16] {'col'}, dimensions={0}, use_global_device_ids=true | all-gather | bytes 17408 | tf_op jit(solution)/shard_map/all_gather | solution.py:99
  30.5 0.9 fusion.40
  31.4 4.1 %collective-permute-start.4 = (f32[5,136,4]{2,1,0:T(8,128)}, f32[5,136,4]{2,1,0:T(8,128)}, u32[]{:S(2)}, u32[]{:S(2)}) collective-permute-start(f32[5,136,4]{2,1,0:T(8,128)} %get-tuple-element.296), channel_id=1, source_target_pairs={{0,1},{1,2},{2,3},{3,4},{4,5},{5,6},{6,7},{7,8},{8,9},{9,10},{10,1... | collective-permute-start | bytes 32648 | tf_op jit(solution)/shard_map/ppermute | solution.py:15
  35.5 1.9 %collective-permute-start.5 = (f32[5,136,4]{2,1,0:T(8,128)}, f32[5,136,4]{2,1,0:T(8,128)}, u32[]{:S(2)}, u32[]{:S(2)}) collective-permute-start(f32[5,136,4]{2,1,0:T(8,128)} %get-tuple-element.297), channel_id=1, source_target_pairs={{1,0},{2,1},{3,2},{4,3},{5,4},{6,5},{7,6},{8,7},{9,8},{10,9},{11,1... | collective-permute-start | bytes 32648 | tf_op jit(solution)/shard_map/ppermute | solution.py:18
  37.5 49.9 %while.32 = (s32[]{:T(128)}, f32[4,1024]{1,0:T(4,128)S(1)}, f32[4,64]{1,0:T(4,128)S(1)}, s32[]{:T(128)}, f32[64,1024]{1,0:T(8,128)S(1)}, /*index=5*/f32[4,64]{1,0:T(4,128)S(1)}, s32[]{:T(128)}, s32[]{:T(128)}) while((s32[]{:T(128)}, f32[4,1024]{1,0:T(4,128)S(1)}, f32[4,64]{1,0:T(4,128)S(1)}, s32[]{:T(128)}, ...), condition=%wide.region_2.3_spmd.clone, body=%wide.region_1.2_spmd.clone.sunk | while | flops 3146500 | bytes 430225 | solution.py:114
  37.8 19.7 %all-gather.7 = f32[16,64,4]{1,2,0:T(4,128)S(1)} all-gather(f32[1,64,4]{1,2,0:T(4,128)S(1)} %bitcast.53), channel_id=1, replica_groups=mesh['row'=2,'col'=16] {'col'}, dimensions={0}, use_global_device_ids=true | all-gather | bytes 17408 | tf_op jit(solution)/shard_map/while/body/eval_jaxpr/all_gather | solution.py:106
  57.6 4.3 %collective-permute-start = (f32[4,1024]{1,0:T(4,128)S(1)}, f32[4,1024]{1,0:T(4,128)S(1)}, u32[]{:S(2)}, u32[]{:S(2)}) collective-permute-start(f32[4,1024]{1,0:T(4,128)S(1)} %bitcast.54), channel_id=1, source_target_pairs={{0,16},{1,17},{2,18},{3,19},{4,20},{5,21},{6,22},{7,23},{8,24},{9,... | collective-permute-start | bytes 49160 | tf_op jit(solution)/shard_map/while/body/eval_jaxpr/ppermute | solution.py:26
  62.9 19.6 %all-gather.7 = f32[16,64,4]{1,2,0:T(4,128)S(1)} all-gather(f32[1,64,4]{1,2,0:T(4,128)S(1)} %bitcast.53), channel_id=1, replica_groups=mesh['row'=2,'col'=16] {'col'}, dimensions={0}, use_global_device_ids=true | all-gather | bytes 17408 | tf_op jit(solution)/shard_map/while/body/eval_jaxpr/all_gather | solution.py:106
  82.6 3.9 %collective-permute-start = (f32[4,1024]{1,0:T(4,128)S(1)}, f32[4,1024]{1,0:T(4,128)S(1)}, u32[]{:S(2)}, u32[]{:S(2)}) collective-permute-start(f32[4,1024]{1,0:T(4,128)S(1)} %bitcast.54), channel_id=1, source_target_pairs={{0,16},{1,17},{2,18},{3,19},{4,20},{5,21},{6,22},{7,23},{8,24},{9,... | collective-permute-start | bytes 49160 | tf_op jit(solution)/shard_map/while/body/eval_jaxpr/ppermute | solution.py:26
  87.4 48.1 %while.33 = (s32[]{:T(128)}, f32[4,1024]{1,0:T(4,128)S(1)}, f32[4,64]{1,0:T(4,128)S(1)}, s32[]{:T(128)}, f32[64,1024]{1,0:T(8,128)S(1)}, /*index=5*/f32[4,64]{1,0:T(4,128)S(1)}, s32[]{:T(128)}, s32[]{:T(128)}) while((s32[]{:T(128)}, f32[4,1024]{1,0:T(4,128)S(1)}, f32[4,64]{1,0:T(4,128)S(1)}, s32[]{:T(128)}, ...), condition=%wide.region_4.5_spmd.clone, body=%wide.region_3.4_spmd.clone.sunk | while | flops 3146501 | bytes 430237 | solution.py:124
  87.7 18.6 %all-gather.8 = f32[16,64,4]{1,2,0:T(4,128)S(1)} all-gather(f32[1,64,4]{1,2,0:T(4,128)S(1)} %bitcast.56), channel_id=1, replica_groups=mesh['row'=2,'col'=16] {'col'}, dimensions={0}, use_global_device_ids=true | all-gather | bytes 17408 | tf_op jit(solution)/shard_map/while/body/eval_jaxpr/all_gather | solution.py:120
  106.3 1.3 collective-permute-start.1
  107.6 3.2 %collective-permute-done.1 = f32[4,1024]{1,0:T(4,128)S(1)} collective-permute-done((f32[4,1024]{1,0:T(4,128)S(1)}, f32[4,1024]{1,0:T(4,128)S(1)}, u32[]{:S(2)}, u32[]{:S(2)}) %collective-permute-start.1) | collective-permute-done | bytes 16416 | tf_op jit(solution)/shard_map/while/body/eval_jaxpr/ppermute | solution.py:26
  111.1 19.9 %all-gather.8 = f32[16,64,4]{1,2,0:T(4,128)S(1)} all-gather(f32[1,64,4]{1,2,0:T(4,128)S(1)} %bitcast.56), channel_id=1, replica_groups=mesh['row'=2,'col'=16] {'col'}, dimensions={0}, use_global_device_ids=true | all-gather | bytes 17408 | tf_op jit(solution)/shard_map/while/body/eval_jaxpr/all_gather | solution.py:120
  131.1 1.3 collective-permute-start.1
  132.3 3.2 %collective-permute-done.1 = f32[4,1024]{1,0:T(4,128)S(1)} collective-permute-done((f32[4,1024]{1,0:T(4,128)S(1)}, f32[4,1024]{1,0:T(4,128)S(1)}, u32[]{:S(2)}, u32[]{:S(2)}) %collective-permute-start.1) | collective-permute-done | bytes 16416 | tf_op jit(solution)/shard_map/while/body/eval_jaxpr/ppermute | solution.py:26
  136.4 1.6 %pad_maximum_fusion = f32[5,136,264]{2,1,0:T(8,128)S(1)} fusion(f32[5,136,4]{2,1,0:T(8,128)} %collective-permute-done.5, f32[5,4,256]{2,1,0:T(4,128)} %copy-done.10, f32[1,128,256]{2,1,0:T(8,128)S(1)} %bitcast.52, f32[4,128,256]{2,1,0:T(8,128)S(1)} %copy-done.1, f32[5,4,256]{2,1,0:T(4,128)} %copy-done.9, f32[5,136,4]{2,1,0:T(8,128)} %collective-permute-done.4), kind=kLoop, calls=%fused_computation.4 | loop fusion | flops 897600 | bytes 1436160 | tf_op jit(solution)/shard_map/concatenate | solution.py:19
  140.2 1.0 fusion.16
  141.2 1.0 fusion.10
  142.2 1.0 fusion.4
  143.2 1.3 fusion.23
  (79 shorter events, 11.6 us)
Async XLA Ops:
  0.0 26.1 %copy-start = (f32[1,64,1024]{2,1,0:T(8,128)S(1)}, f32[1,64,1024]{2,1,0:T(8,128)}, u32[]{:S(2)}) copy-start(f32[1,64,1024]{2,1,0:T(8,128)} %param.11) | copy-start | bytes 786436
  0.9 28.9 %collective-permute-start.2 = (f32[5,4,256]{2,1,0:T(4,128)S(1)}, f32[5,4,256]{2,1,0:T(4,128)S(1)}, u32[]{:S(2)}, u32[]{:S(2)}) collective-permute-start(f32[5,4,256]{2,1,0:T(4,128)S(1)} %get-tuple-element.298), channel_id=1, source_target_pairs={{0,16},{1,17},{2,18},{3,19},{4,20},{5,21},{6,22},{7,23},{8,24},{9,... | collective-permute-start | bytes 61448 | tf_op jit(solution)/shard_map/ppermute | solution.py:15
  4.0 25.8 %collective-permute-start.3 = (f32[5,4,256]{2,1,0:T(4,128)S(1)}, f32[5,4,256]{2,1,0:T(4,128)S(1)}, u32[]{:S(2)}, u32[]{:S(2)}) collective-permute-start(f32[5,4,256]{2,1,0:T(4,128)S(1)} %get-tuple-element.299), channel_id=1, source_target_pairs={{16,0},{17,1},{18,2},{19,3},{20,4},{21,5},{22,6},{23,7},{24,8},{25... | collective-permute-start | bytes 61448 | tf_op jit(solution)/shard_map/ppermute | solution.py:18
  6.9 23.5 %copy-start.1 = (f32[4,128,256]{2,1,0:T(8,128)S(1)}, f32[4,128,256]{2,1,0:T(8,128)}, u32[]{:S(2)}) copy-start(f32[4,128,256]{2,1,0:T(8,128)} %param.9) | copy-start | bytes 1572868
  6.9 23.5 %copy-start.4 = (f32[128,256]{1,0:T(8,128)S(1)}, f32[128,256]{1,0:T(8,128)}, u32[]{:S(2)}) copy-start(f32[128,256]{1,0:T(8,128)} %param.10) | copy-start | bytes 393220
  26.6 10.9 %copy-start.2 = (f32[1,64,1024]{2,1,0:T(8,128)S(1)}, f32[1,64,1024]{2,1,0:T(8,128)}, u32[]{:S(2)}) copy-start(f32[1,64,1024]{2,1,0:T(8,128)} %param.12) | copy-start | bytes 786436
  29.8 7.7 %copy-start.9 = (f32[5,4,256]{2,1,0:T(4,128)}, f32[5,4,256]{2,1,0:T(4,128)S(1)}, u32[]{:S(2)}) copy-start(f32[5,4,256]{2,1,0:T(4,128)S(1)} %collective-permute-done.2) | copy-start | bytes 61444
  29.8 0.6 copy-start.10
  30.5 56.9 %copy-start.3 = (f32[1,64,1024]{2,1,0:T(8,128)S(1)}, f32[1,64,1024]{2,1,0:T(8,128)}, u32[]{:S(2)}) copy-start(f32[1,64,1024]{2,1,0:T(8,128)} %param.13) | copy-start | bytes 786436
  31.4 105.0 %collective-permute-start.4 = (f32[5,136,4]{2,1,0:T(8,128)}, f32[5,136,4]{2,1,0:T(8,128)}, u32[]{:S(2)}, u32[]{:S(2)}) collective-permute-start(f32[5,136,4]{2,1,0:T(8,128)} %get-tuple-element.296), channel_id=1, source_target_pairs={{0,1},{1,2},{2,3},{3,4},{4,5},{5,6},{6,7},{7,8},{8,9},{9,10},{10,1... | collective-permute-start | bytes 32648 | tf_op jit(solution)/shard_map/ppermute | solution.py:15
  35.5 100.9 %collective-permute-start.5 = (f32[5,136,4]{2,1,0:T(8,128)}, f32[5,136,4]{2,1,0:T(8,128)}, u32[]{:S(2)}, u32[]{:S(2)}) collective-permute-start(f32[5,136,4]{2,1,0:T(8,128)} %get-tuple-element.297), channel_id=1, source_target_pairs={{1,0},{2,1},{3,2},{4,3},{5,4},{6,5},{7,6},{8,7},{9,8},{10,9},{11,1... | collective-permute-start | bytes 32648 | tf_op jit(solution)/shard_map/ppermute | solution.py:18
  57.6 5.1 %collective-permute-start = (f32[4,1024]{1,0:T(4,128)S(1)}, f32[4,1024]{1,0:T(4,128)S(1)}, u32[]{:S(2)}, u32[]{:S(2)}) collective-permute-start(f32[4,1024]{1,0:T(4,128)S(1)} %bitcast.54), channel_id=1, source_target_pairs={{0,16},{1,17},{2,18},{3,19},{4,20},{5,21},{6,22},{7,23},{8,24},{9,... | collective-permute-start | bytes 49160 | tf_op jit(solution)/shard_map/while/body/eval_jaxpr/ppermute | solution.py:26
  82.6 4.8 %collective-permute-start = (f32[4,1024]{1,0:T(4,128)S(1)}, f32[4,1024]{1,0:T(4,128)S(1)}, u32[]{:S(2)}, u32[]{:S(2)}) collective-permute-start(f32[4,1024]{1,0:T(4,128)S(1)} %bitcast.54), channel_id=1, source_target_pairs={{0,16},{1,17},{2,18},{3,19},{4,20},{5,21},{6,22},{7,23},{8,24},{9,... | collective-permute-start | bytes 49160 | tf_op jit(solution)/shard_map/while/body/eval_jaxpr/ppermute | solution.py:26
  106.3 4.5 %collective-permute-start.1 = (f32[4,1024]{1,0:T(4,128)S(1)}, f32[4,1024]{1,0:T(4,128)S(1)}, u32[]{:S(2)}, u32[]{:S(2)}) collective-permute-start(f32[4,1024]{1,0:T(4,128)S(1)} %bitcast.55), channel_id=1, source_target_pairs={{16,0},{17,1},{18,2},{19,3},{20,4},{21,5},{22,6},{23,7},{24,8},{25... | collective-permute-start | bytes 49160 | tf_op jit(solution)/shard_map/while/body/eval_jaxpr/ppermute | solution.py:26
  131.1 4.5 %collective-permute-start.1 = (f32[4,1024]{1,0:T(4,128)S(1)}, f32[4,1024]{1,0:T(4,128)S(1)}, u32[]{:S(2)}, u32[]{:S(2)}) collective-permute-start(f32[4,1024]{1,0:T(4,128)S(1)} %bitcast.55), channel_id=1, source_target_pairs={{16,0},{17,1},{18,2},{19,3},{20,4},{21,5},{22,6},{23,7},{24,8},{25... | collective-permute-start | bytes 49160 | tf_op jit(solution)/shard_map/while/body/eval_jaxpr/ppermute | solution.py:26
  138.7 1.4 copy-start.7
  140.2 1.0 copy-start.6
  141.2 1.0 copy-start.5
  142.2 1.0 copy-start.8
where the time goes:
time: 147 us; the launch traced here: 144 us
  blocking collectives  96.5 us (66%)
  starting transfers between devices  21.1 us (14%)
  local copies, waits for them, and re-layouts  9.48 us (6%)
  waiting for transfers between devices  8.07 us (5%)
  other arithmetic  7.39 us (5%)
    all_gather x2, blocking collectives, forward_turn(): gathered = lax.all_gather(stored, 'col', axis=1, tiled=True)  39.3 us
    all_gather x2, blocking collectives, backward_turn(): gathered = lax.all_gather(stored, 'col', axis=1, tiled=True)  38.4 us
    all_gather x1, blocking collectives, on_device(): coarse_full = lax.all_gather(coarse, 'col', axis=1, tiled=True)  18.8 us
    ppermute x4, starting transfers between devices, from_behind(): lax.ppermute(value, axis, [(source, source + steps) for source in range(f...  10.7 us
    ppermute x4, waiting for transfers between devices, from_behind(): lax.ppermute(value, axis, [(source, source + steps) for source in range(f...  8.05 us
    ppermute x2, starting transfers between devices, extended(): lax.ppermute(lax.slice_in_dim(block, block.shape[dim] - width, None, axis...  7.21 us
    slice x19, local copies, waits for them, and re-layouts, crop_region(): return array[..., offset:offset + extent_x, offset:offset + extent_y]  4.87 us
    ppermute x2, starting transfers between devices, extended(): lax.ppermute(lax.slice_in_dim(block, 0, width, axis=dim), axis, backward)  3.21 us
  transfers between devices with their start and end apart: 8, of which 4 were waited for; matrix products, arithmetic and copies ran while one was open for 6% of the time, Pallas kernels for 0%

commit v1 on v0

v1 whole, which is shorter than its diff:
```python
import functools

import jax
import jax.numpy as jnp
from jax import lax
from jax.experimental import pallas as pl
from jax.experimental.pallas import tpu as pltpu
from jax.sharding import PartitionSpec as P

SWEEPS = 4
SUB = 8
LANES = 128
TILE = 8
VMEM = pl.BlockSpec(memory_space=pltpu.VMEM)
HIGHEST = lax.Precision.HIGHEST


def params():
    return pltpu.CompilerParams(vmem_limit_bytes=16 * 1024 * 1024)


def call(kernel, name, outs, scratch=(), flops=1_000_000):
    return pl.pallas_call(
        kernel,
        out_shape=outs,
        scratch_shapes=list(scratch),
        compiler_params=params(),
        cost_estimate=pl.CostEstimate(flops=flops, bytes_accessed=1_000_000, transcendentals=0),
        name=name,
    )


def f32(*shape):
    return jax.ShapeDtypeStruct(shape, jnp.float32)


def iota(shape, dim):
    return lax.broadcasted_iota(jnp.int32, shape, dim)


def thirds(value):
    first = value.astype(jnp.bfloat16)
    rest = value - first.astype(jnp.float32)
    second = rest.astype(jnp.bfloat16)
    third = (rest - second.astype(jnp.float32)).astype(jnp.bfloat16)
    return first, second, third


def selected(value, selector):
    return sum(
        jnp.dot(part, selector, preferred_element_type=jnp.float32) for part in thirds(value)
    )


def restrict_kernel(rhs_ref, coupling_ref, block_ref, low_ref, high_ref):
    count, extent_x, extent_y = rhs_ref.shape
    own = SUB * SUB
    pack = LANES // own
    sub_x, sub_y = extent_x // SUB, extent_y // SUB
    parts = []
    for b in range(count):
        cells = rhs_ref[b].reshape(SUB, sub_x // TILE, TILE, extent_y).sum(axis=1)
        parts.append(cells.reshape(SUB * TILE, extent_y))
    stacked = jnp.concatenate(parts, axis=0)
    shape = (extent_y, LANES)
    selector = (iota(shape, 0) // sub_y == iota(shape, 1) % SUB).astype(jnp.bfloat16)
    sums = selected(stacked, selector).reshape(count, SUB * TILE, LANES)
    lane = iota(sums.shape, 2)
    keep = (iota(sums.shape, 1) // TILE == (lane % own) // SUB) & (
        lane // own == lax.axis_index("col") % pack
    )
    block = jnp.where(keep, sums, 0.0).sum(axis=1) * (1.0 / (sub_x * sub_y))
    block_ref[...] = jnp.broadcast_to(block[None], block_ref.shape)
    for b in range(count + 1):
        field = rhs_ref.at[b] if b < count else coupling_ref
        low_ref[b] = field[:SWEEPS, :]
        high_ref[b] = field[extent_x - SWEEPS :, :]


def joined(gathered_ref, first, members, pack):
    blocks = []
    for p in range(members // pack):
        total = gathered_ref[first + pack * p]
        for q in range(1, pack):
            total = total + gathered_ref[first + pack * p + q]
        blocks.append(total)
    return jnp.concatenate(blocks, axis=1)


def product(gathered_ref, matrix_ref, offset):
    own, block = matrix_ref.shape[1:]
    members = block // own
    rows = gathered_ref.shape[0] // members
    first = 0
    if rows > 1:
        first = (lax.axis_index("row") + rows + offset) % rows * members
    values = joined(gathered_ref, first, members, LANES // own)
    return lax.dot_general(
        values,
        matrix_ref[0],
        (((1,), (1,)), ((), ())),
        precision=HIGHEST,
        preferred_element_type=jnp.float32,
    )


def place(own_values, block_ref):
    own = own_values.shape[1]
    pack = LANES // own
    wide = jnp.concatenate([own_values] * pack, axis=1)
    keep = iota(wide.shape, 1) // own == lax.axis_index("col") % pack
    block_ref[...] = jnp.broadcast_to(jnp.where(keep, wide, 0.0)[None], block_ref.shape)


def drive_kernel(gathered_ref, pivot_ref, own_ref, block_ref):
    values = product(gathered_ref, pivot_ref, 0)
    own_ref[...] = values
    place(values, block_ref)


def turn_kernel(turn, offset, gathered_ref, factor_ref, base_ref, stored_ref, own_ref, block_ref):
    update = base_ref[...] - product(gathered_ref, factor_ref, offset)
    values = jnp.where(lax.axis_index("row") == turn, update, stored_ref[...])
    own_ref[...] = values
    place(values, block_ref)


def finish_kernel(turn, gathered_ref, factor_ref, base_ref, stored_ref, fine_ref, out_ref):
    values = stored_ref[...]
    if turn is not None:
        update = base_ref[...] - product(gathered_ref, factor_ref, 1)
        values = jnp.where(lax.axis_index("row") == turn, update, values)
    count, extent_x, extent_y = fine_ref.shape
    own = values.shape[1]
    sub_x, sub_y = extent_x // SUB, extent_y // SUB
    spread = jnp.broadcast_to(values[:, None, :], (count, SUB, own))
    spread = jnp.where(iota(spread.shape, 2) // SUB == iota(spread.shape, 1), spread, 0.0)
    shape = (own, extent_y)
    selector = (iota(shape, 0) % SUB == iota(shape, 1) // sub_y).astype(jnp.bfloat16)
    coarse = selected(spread.reshape(count * SUB, own), selector)
    for b in range(count):
        for r in range(SUB):
            line = coarse[b * SUB + r : b * SUB + r + 1, :]
            rows = slice(r * sub_x, (r + 1) * sub_x)
            out_ref[b, rows, :] = fine_ref[b, rows, :] + line


def pack_kernel(rhs_ref, coupling_ref, above_ref, below_ref, first_ref, last_ref):
    count, extent_x, extent_y = rhs_ref.shape
    tiles = extent_x // TILE
    lane = iota((TILE, LANES), 1)
    for b in range(count + 1):
        field = rhs_ref.at[b] if b < count else coupling_ref
        halo = jnp.concatenate([below_ref[b], above_ref[b]], axis=0)
        for target, start, edge in (
            (first_ref, 0, 0),
            (last_ref, extent_y - LANES, LANES - SWEEPS),
        ):
            packed = jnp.zeros((TILE, LANES), jnp.float32)
            for i in range(tiles + 1):
                if i < tiles:
                    tile = field[i * TILE : (i + 1) * TILE, start : start + LANES]
                else:
                    tile = halo[:, start : start + LANES]
                shift = (SWEEPS * i - edge) % LANES
                moved = pltpu.roll(tile, shift, 1) if shift else tile
                packed = jnp.where(lane // SWEEPS == i, moved, packed)
            target[b] = packed


def shifted(ref, index, t):
    width = ref.shape[-1]
    here = ref[index, pl.ds(pl.multiple_of(t * TILE, TILE), TILE), :]
    before = ref[index, pl.ds(pl.multiple_of((t - 1) * TILE, TILE), TILE), :]
    after = ref[index, pl.ds(pl.multiple_of((t + 1) * TILE, TILE), TILE), :]
    sub = iota(here.shape, 0)
    up = jnp.where(sub == 0, pltpu.roll(before, 1, 0), pltpu.roll(here, 1, 0))
    down = jnp.where(
        sub == TILE - 1, pltpu.roll(after, TILE - 1, 0), pltpu.roll(here, TILE - 1, 0)
    )
    left = pltpu.roll(here, 1, 1)
    right = pltpu.roll(here, width - 1, 1)
    return here, up, down, left, right


def fine_kernel(
    rhs_ref, coupling_ref, above_ref, below_ref, left_ref, right_ref, out_ref,
    first_ref, second_ref, scaled_ref, face_ref,
):
    count, extent_x, extent_y = rhs_ref.shape
    tiles = extent_x // TILE
    width = extent_y + LANES
    lane = iota((TILE, LANES), 1)
    sub = iota((TILE, LANES), 0)
    blank = jnp.zeros((TILE, width), jnp.float32)
    for b in range(count + 1):
        field = rhs_ref.at[b] if b < count else coupling_ref
        for edge in (0, tiles + 3):
            first_ref[b, edge * TILE : (edge + 1) * TILE, :] = blank
            if b < count:
                second_ref[b, edge * TILE : (edge + 1) * TILE, :] = blank
        none = jnp.zeros((SWEEPS, extent_y), jnp.float32)
        first_ref[b, TILE : 2 * TILE, :extent_y] = jnp.concatenate([none, above_ref[b]], axis=0)
        first_ref[b, 2 * TILE : (2 + tiles) * TILE, :extent_y] = field[...]
        last = (2 + tiles) * TILE
        first_ref[b, last : last + TILE, :extent_y] = jnp.concatenate([below_ref[b], none], axis=0)
        for i in range(tiles + 1):
            low = pltpu.roll(right_ref[b], (-SWEEPS * i) % LANES, 1) if i else right_ref[b]
            high = pltpu.roll(left_ref[b], (LANES - SWEEPS - SWEEPS * i) % LANES, 1)
            tile = jnp.where(lane < SWEEPS, low, jnp.where(lane >= LANES - SWEEPS, high, 0.0))
            if i < tiles:
                place_at = (2 + i) * TILE
                first_ref[b, place_at : place_at + TILE, extent_y:] = tile
            else:
                half = TILE // 2
                first_ref[b, TILE : 2 * TILE, extent_y:] = jnp.where(sub >= half, tile, 0.0)
                first_ref[b, last : last + TILE, extent_y:] = jnp.where(sub < half, tile, 0.0)

    total_x = extent_x * lax.axis_size("row")
    total_y = extent_y * lax.axis_size("col")
    wide = (TILE, width)
    column = iota(wide, 1)
    own_y = jnp.where(column < extent_y + SWEEPS, column, column - width)
    global_y = own_y + lax.axis_index("col") * extent_y
    inside_y = (own_y >= -SWEEPS) & (global_y >= 0) & (global_y < total_y)

    def prepare(t, unused):
        here, up, down, left, right = shifted(first_ref, count, t)
        up = 0.5 * (here + up)
        down = 0.5 * (here + down)
        left = 0.5 * (here + left)
        right = 0.5 * (here + right)
        diagonal = 1.0 + up + down + left + right
        global_x = lax.axis_index("row") * extent_x + (t - 2) * TILE + iota(wide, 0)
        inside = inside_y & (global_x >= 0) & (global_x < total_x)
        inverse = jnp.where(inside, 1.0, 0.0) / diagonal
        rows = pl.ds(pl.multiple_of(t * TILE, TILE), TILE)
        for index, face in enumerate((up, down, left, right)):
            face_ref[index, rows, :] = face * inverse
        for b in range(count):
            scaled_ref[b, rows, :] = first_ref[b, rows, :] * inverse
        return unused

    lax.fori_loop(1, tiles + 3, prepare, 0)

    def relax(source, t, b):
        rows = pl.ds(pl.multiple_of(t * TILE, TILE), TILE)
        here, up, down, left, right = shifted(source, b, t)
        total = scaled_ref[b, rows, :] + face_ref[0, rows, :] * up
        total = total + face_ref[1, rows, :] * down
        total = total + face_ref[2, rows, :] * left
        return total + face_ref[3, rows, :] * right

    buffers = (first_ref, second_ref)
    for sweep in range(SWEEPS - 1):
        source, target = buffers[sweep % 2], buffers[(sweep + 1) % 2]

        def step(t, unused, source=source, target=target):
            rows = pl.ds(pl.multiple_of(t * TILE, TILE), TILE)
            for b in range(count):
                target[b, rows, :] = relax(source, t, b)
            return unused

        lax.fori_loop(1, tiles + 3, step, 0)

    def close(t, unused):
        rows = pl.ds(pl.multiple_of((t - 2) * TILE, TILE), TILE)
        for b in range(count):
            out_ref[b, rows, :] = relax(buffers[(SWEEPS - 1) % 2], t, b)[:, :extent_y]
        return unused

    lax.fori_loop(2, tiles + 2, close, 0)


def on_device(rhs_fields, coupling, inv_pivot, lower_factor, upper_factor):
    count, extent_x, extent_y = rhs_fields.shape
    own, block = inv_pivot.shape[1:]
    rows, columns = lax.axis_size("row"), lax.axis_size("col")
    row = lax.axis_index("row")
    both = ("row", "col")

    coarse, low, high = call(
        restrict_kernel,
        "restrict",
        (
            f32(columns, count, LANES),
            f32(count + 1, SWEEPS, extent_y),
            f32(count + 1, SWEEPS, extent_y),
        ),
    )(rhs_fields, coupling)
    gathered = lax.all_to_all(coarse, "col", 0, 0)

    if rows == 2:
        other = lax.ppermute(jnp.where(row == 0, high, low), "row", [(0, 1), (1, 0)])
        above = jnp.where(row == 0, 0.0, other)
        below = jnp.where(row == 0, other, 0.0)
    else:
        above = lax.ppermute(high, "row", [(i, i + 1) for i in range(rows - 1)])
        below = lax.ppermute(low, "row", [(i + 1, i) for i in range(rows - 1)])
    edge = f32(count + 1, TILE, LANES)
    first, last = call(pack_kernel, "pack", (edge, edge))(rhs_fields, coupling, above, below)
    left = lax.ppermute(last, "col", [(i, i + 1) for i in range(columns - 1)])
    right = lax.ppermute(first, "col", [(i + 1, i) for i in range(columns - 1)])
    tall = extent_x + 4 * TILE
    wide = extent_y + LANES
    fine = call(
        fine_kernel,
        "fine",
        f32(count, extent_x, extent_y),
        (
            pltpu.VMEM((count + 1, tall, wide), jnp.float32),
            pltpu.VMEM((count, tall, wide), jnp.float32),
            pltpu.VMEM((count, tall, wide), jnp.float32),
            pltpu.VMEM((4, tall, wide), jnp.float32),
        ),
        flops=20_000_000,
    )(rhs_fields, coupling, above, below, left, right)

    results = (f32(count, own), f32(rows * columns, count, LANES))
    driven, blocks = call(drive_kernel, "drive", results)(gathered, inv_pivot)
    stored = driven
    for turn in range(1, rows):
        gathered = lax.all_to_all(blocks, both, 0, 0)
        stored, blocks = call(
            functools.partial(turn_kernel, turn, -1), f"forward{turn}", results
        )(gathered, lower_factor, driven, stored)
    downs = stored
    for turn in range(rows - 2, 0, -1):
        gathered = lax.all_to_all(blocks, both, 0, 0)
        stored, blocks = call(
            functools.partial(turn_kernel, turn, 1), f"backward{turn}", results
        )(gathered, upper_factor, downs, stored)
    last_turn = None
    if rows > 1:
        gathered = lax.all_to_all(blocks, both, 0, 0)
        last_turn = 0
    return call(
        functools.partial(finish_kernel, last_turn), "finish", f32(count, extent_x, extent_y)
    )(gathered, upper_factor, downs, stored, fine)


def solution(mesh):
    return jax.shard_map(
        on_device,
        mesh=mesh,
        in_specs=(
            P(None, "row", "col"),
            P("row", "col"),
            P("row", "col", None),
            P("row", "col", None),
            P("row", "col", None),
        ),
        out_specs=P(None, "row", "col"),
        check_vma=False,
    )
```

time: 147 us -> 51.1 us (0.35); the launches traced: 144 us -> 50.7 us
  blocking collectives: 96.5 us -> 0 us
  Pallas kernels: 0 us -> 13.3 us
  local copies, waits for them, and re-layouts: 9.48 us -> 1.97 us
  other arithmetic: 7.39 us -> 0.02 us
  waiting for transfers between devices: 8.07 us -> 14 us
    all_gather x5 -> x0, blocking collectives: 96.5 us -> none  [the longest x2 39.3 us: forward_turn(): gathered = lax.all_gather(stored, 'col', axis=1, tiled=True)]
    all_to_all x0 -> x3, starting transfers between devices: none -> 14.6 us  [the longest x2 7.8 us: on_device(): gathered = lax.all_to_all(blocks, both, 0, 0)]
    ppermute x8 -> x3, starting transfers between devices: 21.1 us -> 6.71 us  [the longest x1 3.4 us: on_device(): left = lax.ppermute(last, 'col', [(i, i + 1) for i in range(columns - 1)])]
    pallas_call x0 -> x6, Pallas kernels: none -> 13.3 us  [the longest x1 8.77 us: on_device(): call(fine_kernel, 'fine', f32(count, extent_x, extent_y), (pltpu.VMEM((co...]
    all_to_all x0 -> x3, waiting for transfers between devices: none -> 9.96 us  [the longest x1 5.04 us: on_device(): gathered = lax.all_to_all(coarse, 'col', 0, 0)]
    slice x20 -> x0, local copies, waits for them, and re-layouts: 5.81 us -> none  [the longest x19 4.87 us: crop_region(): return array[..., offset:offset + extent_x, offset:offset + extent_y]]
    ppermute x8 -> x3, waiting for transfers between devices: 8.07 us -> 4.07 us  [the longest x1 4.06 us: on_device(): right = lax.ppermute(first, 'col', [(i + 1, i) for i in range(columns - 1)])]
    mul x3 -> x0, other arithmetic: 2.92 us -> none  [on_device(): fine = fine * crop_region(inside, repeat + 1, size_x, size_y)]
  transfers between devices with their start and end apart: 8 -> 6, of which waited for: 4 -> 3; matrix products, arithmetic and copies ran while one was open for 6% -> 0% of each run, Pallas kernels for 0% -> 20%
where the time goes in v1:
time: 51.1 us; the launch traced here: 50.7 us
  starting transfers between devices  21.3 us (42%)
  waiting for transfers between devices  14 us (27%)
  Pallas kernels  13.3 us (26%)
  local copies, waits for them, and re-layouts  1.97 us (4%)
    pallas_call x1, Pallas kernels, on_device(): call(fine_kernel, 'fine', f32(count, extent_x, extent_y), (pltpu.VMEM((co...  8.77 us
    all_to_all x2, starting transfers between devices, on_device(): gathered = lax.all_to_all(blocks, both, 0, 0)  7.8 us
    all_to_all x1, starting transfers between devices, on_device(): gathered = lax.all_to_all(coarse, 'col', 0, 0)  6.76 us
    all_to_all x1, waiting for transfers between devices, on_device(): gathered = lax.all_to_all(coarse, 'col', 0, 0)  5.04 us
    all_to_all x2, waiting for transfers between devices, on_device(): gathered = lax.all_to_all(blocks, both, 0, 0)  4.92 us
    ppermute x1, waiting for transfers between devices, on_device(): right = lax.ppermute(first, 'col', [(i + 1, i) for i in range(columns - 1)])  4.06 us
    ppermute x1, starting transfers between devices, on_device(): left = lax.ppermute(last, 'col', [(i, i + 1) for i in range(columns - 1)])  3.4 us
    ppermute x1, starting transfers between devices, on_device(): right = lax.ppermute(first, 'col', [(i + 1, i) for i in range(columns - 1)])  2.05 us
  transfers between devices with their start and end apart: 6, of which 3 were waited for; matrix products, arithmetic and copies ran while one was open for 0% of the time, Pallas kernels for 20%

profile of v1, /device:TPU:5, one launch (start us, length us, event | category | flops | bytes accessed | tf_op | source)
XLA Modules:
  0.0 50.7 jit_solution(5842193050881917662)
XLA Ops:
  0.0 1.0 %copy-done = f32[4,128,256]{2,1,0:T(8,128)S(1)} copy-done((f32[4,128,256]{2,1,0:T(8,128)S(1)}, f32[4,128,256]{2,1,0:T(8,128)}, u32[]{:S(2)}) %copy-start) | copy-done | bytes 524312
  1.0 0.9 %copy-done.2 = f32[128,256]{1,0:T(8,128)S(1)} copy-done((f32[128,256]{1,0:T(8,128)S(1)}, f32[128,256]{1,0:T(8,128)}, u32[]{:S(2)}) %copy-start.2) | copy-done | bytes 131096
  1.9 0.9 %restrict.1 = (f32[16,4,128]{2,1,0:T(4,128)}, f32[5,4,256]{2,1,0:T(4,128)S(1)}, f32[5,4,256]{2,1,0:T(4,128)S(1)}) custom-call(f32[4,128,256]{2,1,0:T(8,128)S(1)} %copy-done, f32[128,256]{1,0:T(8,128)S(1)} %copy-done.2), custom_call_target="tpu_custom_call" | custom-call | flops 1000000 | bytes 1000000 | tf_op jit(solution)/shard_map/restrict/pallas_call | solution.py:282
  2.8 6.8 %all-to-all-start = ((f32[16,4,128]{2,1,0:T(4,128)}), f32[16,4,128]{2,1,0:T(4,128)S(1)}, u32[]{:S(2)}, u32[]{:S(2)}) async-start(f32[16,4,128]{2,1,0:T(4,128)} %get-tuple-element.14), calls=%async_computation | async-start | bytes 65536 | tf_op jit(solution)/shard_map/all_to_all | solution.py:291
  9.6 5.0 %all-to-all-done.gathered_ref = f32[16,4,128]{2,1,0:T(4,128)S(1)} async-done(((f32[16,4,128]{2,1,0:T(4,128)}), f32[16,4,128]{2,1,0:T(4,128)S(1)}, u32[]{:S(2)}, u32[]{:S(2)}) %all-to-all-start) | async-done | bytes 32800 | tf_op jit(solution)/shard_map/all_to_all | solution.py:291
  14.7 1.0 %drive.1 = (f32[4,64]{1,0:T(4,128)S(1)}, f32[32,4,128]{2,1,0:T(4,128)}) custom-call(f32[16,4,128]{2,1,0:T(4,128)S(1)} %all-to-all-done.gathered_ref, f32[1,64,1024]{2,1,0:T(8,128)S(1)} %copy-done.4), custom_call_target="tpu_custom_call" | custom-call | flops 1000000 | bytes 1000000 | tf_op jit(solution)/shard_map/drive/pallas_call | solution.py:320
  15.7 3.9 %all-to-all-start.1 = ((f32[32,4,128]{2,1,0:T(4,128)}), f32[32,4,128]{2,1,0:T(4,128)S(1)}, u32[]{:S(2)}, u32[]{:S(2)}) async-start(f32[32,4,128]{2,1,0:T(4,128)} %get-tuple-element.15), calls=%async_computation.1 | async-start | bytes 131072 | tf_op jit(solution)/shard_map/all_to_all | solution.py:323
  19.6 1.3 %collective-permute-start = (f32[5,4,256]{2,1,0:T(4,128)S(1)}, f32[5,4,256]{2,1,0:T(4,128)S(1)}, u32[]{:S(2)}, u32[]{:S(2)}) collective-permute-start(f32[5,4,256]{2,1,0:T(4,128)S(1)} %broadcast_select_fusion.2), channel_id=1, source_target_pairs={{0,16},{16,0},{1,17},{17,1},{2,18},{18,2},{3,19},{19,3},{4,20},{20... | collective-permute-start | bytes 61448 | tf_op jit(solution)/shard_map/ppermute | solution.py:294
  20.9 4.9 %all-to-all-done.1.gathered_ref = f32[32,4,128]{2,1,0:T(4,128)S(1)} async-done(((f32[32,4,128]{2,1,0:T(4,128)}), f32[32,4,128]{2,1,0:T(4,128)S(1)}, u32[]{:S(2)}, u32[]{:S(2)}) %all-to-all-start.1) | async-done | bytes 65568 | tf_op jit(solution)/shard_map/all_to_all | solution.py:323
  25.8 0.0 copy-done.5
  25.8 1.0 %forward1.1 = (f32[4,64]{1,0:T(4,128)S(1)}, f32[32,4,128]{2,1,0:T(4,128)}) custom-call(f32[32,4,128]{2,1,0:T(4,128)S(1)} %all-to-all-done.1.gathered_ref, f32[1,64,1024]{2,1,0:T(8,128)S(1)} %copy-done.5, f32[4,64]{1,0:T(4,128)S(1)} %get-tuple-element.16.base_ref.stored_ref, f32[4,64]{1,0:T(4,128)S(1)} %get-tuple-element.16.base_ref.stored_ref), custom_call_target="tpu_custom_call" | custom-call | flops 1000000 | bytes 1000000 | tf_op jit(solution)/shard_map/forward1/pallas_call | solution.py:324
  26.8 3.9 %all-to-all-start.2 = ((f32[32,4,128]{2,1,0:T(4,128)}), f32[32,4,128]{2,1,0:T(4,128)S(1)}, u32[]{:S(2)}, u32[]{:S(2)}) async-start(f32[32,4,128]{2,1,0:T(4,128)} %get-tuple-element.17), calls=%async_computation.2 | async-start | bytes 131072 | tf_op jit(solution)/shard_map/all_to_all | solution.py:335
  30.7 0.0 collective-permute-done
  30.8 0.0 copy-done.1
  30.8 0.0 copy-done.3
  30.8 0.2 pack.1
  31.0 3.4 %collective-permute-start.1 = (f32[5,8,128]{2,1,0:T(8,128)S(1)}, f32[5,8,128]{2,1,0:T(8,128)S(1)}, u32[]{:S(2)}, u32[]{:S(2)}) collective-permute-start(f32[5,8,128]{2,1,0:T(8,128)S(1)} %get-tuple-element.21), channel_id=1, source_target_pairs={{0,1},{1,2},{2,3},{3,4},{4,5},{5,6},{6,7},{7,8},{8,9},{9,10},{10,1... | collective-permute-start | bytes 61448 | tf_op jit(solution)/shard_map/ppermute | solution.py:302
  34.4 0.0 copy-start.6
  34.5 2.1 %collective-permute-start.2 = (f32[5,8,128]{2,1,0:T(8,128)S(1)}, f32[5,8,128]{2,1,0:T(8,128)S(1)}, u32[]{:S(2)}, u32[]{:S(2)}) collective-permute-start(f32[5,8,128]{2,1,0:T(8,128)S(1)} %get-tuple-element.22), channel_id=1, source_target_pairs={{1,0},{2,1},{3,2},{4,3},{5,4},{6,5},{7,6},{8,7},{9,8},{10,9},{11,1... | collective-permute-start | bytes 61448 | tf_op jit(solution)/shard_map/ppermute | solution.py:303
  36.5 0.0 collective-permute-done.1.left_ref
  36.5 4.1 %collective-permute-done.2.right_ref = f32[5,8,128]{2,1,0:T(8,128)S(1)} collective-permute-done((f32[5,8,128]{2,1,0:T(8,128)S(1)}, f32[5,8,128]{2,1,0:T(8,128)S(1)}, u32[]{:S(2)}, u32[]{:S(2)}) %collective-permute-start.2) | collective-permute-done | bytes 20512 | tf_op jit(solution)/shard_map/ppermute | solution.py:303
  40.6 8.8 %fine.1.fine_ref = f32[4,128,256]{2,1,0:T(8,128)S(1)} custom-call(f32[4,128,256]{2,1,0:T(8,128)S(1)} %copy-done.1, f32[128,256]{1,0:T(8,128)S(1)} %copy-done.3, f32[5,4,256]{2,1,0:T(4,128)S(1)} %get-tuple-element.24.above_ref, f32[5,4,256]{2,1,0:T(4,128)S(1)} %get-tuple-element.23.below_ref, f32[5,8,128]{2,1,0:T(8,128)S(1)} %collective-permute-done.1.left_ref, ...), custom_call_target="tpu_custom_call" | custom-call | flops 20000000 | bytes 1000000 | tf_op jit(solution)/shard_map/fine/pallas_call | solution.py:306
  49.4 0.0 all-to-all-done.2.gathered_ref
  49.4 1.3 %finish.1 = f32[4,128,256]{2,1,0:T(8,128)} custom-call(f32[32,4,128]{2,1,0:T(4,128)S(1)} %all-to-all-done.2.gathered_ref, f32[1,64,1024]{2,1,0:T(8,128)S(1)} %copy-done.6, f32[4,64]{1,0:T(4,128)S(1)} %get-tuple-element.18.base_ref.stored_ref, f32[4,64]{1,0:T(4,128)S(1)} %get-tuple-element.18.base_ref.stored_ref, f32[4,128,256]{2,1,0:T(8,128)S(1)} %fine.1.fine_ref), custom_call_target="tpu_custom_call" | custom-call | flops 1000000 | bytes 1000000 | tf_op jit(solution)/shard_map/finish/pallas_call | solution.py:337
  (10 shorter events, 0.0 us)
Async XLA Ops:
  0.0 1.0 %copy-start = (f32[4,128,256]{2,1,0:T(8,128)S(1)}, f32[4,128,256]{2,1,0:T(8,128)}, u32[]{:S(2)}) copy-start(f32[4,128,256]{2,1,0:T(8,128)} %rhs_ref.5) | copy-start | bytes 1572868
  1.0 0.9 %copy-start.2 = (f32[128,256]{1,0:T(8,128)S(1)}, f32[128,256]{1,0:T(8,128)}, u32[]{:S(2)}) copy-start(f32[128,256]{1,0:T(8,128)} %coupling_ref.5) | copy-start | bytes 393220
  1.9 12.7 %copy-start.4 = (f32[1,64,1024]{2,1,0:T(8,128)S(1)}, f32[1,64,1024]{2,1,0:T(8,128)}, u32[]{:S(2)}) copy-start(f32[1,64,1024]{2,1,0:T(8,128)} %pivot_ref.1) | copy-start | bytes 786436
  2.8 22.9 %copy-start.5 = (f32[1,64,1024]{2,1,0:T(8,128)S(1)}, f32[1,64,1024]{2,1,0:T(8,128)}, u32[]{:S(2)}) copy-start(f32[1,64,1024]{2,1,0:T(8,128)} %factor_ref.2) | copy-start | bytes 786436
  2.8 11.8 %all-to-all-start = ((f32[16,4,128]{2,1,0:T(4,128)}), f32[16,4,128]{2,1,0:T(4,128)S(1)}, u32[]{:S(2)}, u32[]{:S(2)}) async-start(f32[16,4,128]{2,1,0:T(4,128)} %get-tuple-element.14), calls=%async_computation | async-start | bytes 65536 | tf_op jit(solution)/shard_map/all_to_all | solution.py:291
  9.6 21.2 %copy-start.1 = (f32[4,128,256]{2,1,0:T(8,128)S(1)}, f32[4,128,256]{2,1,0:T(8,128)}, u32[]{:S(2)}) copy-start(f32[4,128,256]{2,1,0:T(8,128)} %rhs_ref.5) | copy-start | bytes 1572868
  15.7 10.1 %all-to-all-start.1 = ((f32[32,4,128]{2,1,0:T(4,128)}), f32[32,4,128]{2,1,0:T(4,128)S(1)}, u32[]{:S(2)}, u32[]{:S(2)}) async-start(f32[32,4,128]{2,1,0:T(4,128)} %get-tuple-element.15), calls=%async_computation.1 | async-start | bytes 131072 | tf_op jit(solution)/shard_map/all_to_all | solution.py:323
  19.6 11.1 %collective-permute-start = (f32[5,4,256]{2,1,0:T(4,128)S(1)}, f32[5,4,256]{2,1,0:T(4,128)S(1)}, u32[]{:S(2)}, u32[]{:S(2)}) collective-permute-start(f32[5,4,256]{2,1,0:T(4,128)S(1)} %broadcast_select_fusion.2), channel_id=1, source_target_pairs={{0,16},{16,0},{1,17},{17,1},{2,18},{18,2},{3,19},{19,3},{4,20},{20... | collective-permute-start | bytes 61448 | tf_op jit(solution)/shard_map/ppermute | solution.py:294
  26.8 4.0 %copy-start.3 = (f32[128,256]{1,0:T(8,128)S(1)}, f32[128,256]{1,0:T(8,128)}, u32[]{:S(2)}) copy-start(f32[128,256]{1,0:T(8,128)} %coupling_ref.5) | copy-start | bytes 393220
  26.8 22.5 %all-to-all-start.2 = ((f32[32,4,128]{2,1,0:T(4,128)}), f32[32,4,128]{2,1,0:T(4,128)S(1)}, u32[]{:S(2)}, u32[]{:S(2)}) async-start(f32[32,4,128]{2,1,0:T(4,128)} %get-tuple-element.17), calls=%async_computation.2 | async-start | bytes 131072 | tf_op jit(solution)/shard_map/all_to_all | solution.py:335
  31.0 5.5 %collective-permute-start.1 = (f32[5,8,128]{2,1,0:T(8,128)S(1)}, f32[5,8,128]{2,1,0:T(8,128)S(1)}, u32[]{:S(2)}, u32[]{:S(2)}) collective-permute-start(f32[5,8,128]{2,1,0:T(8,128)S(1)} %get-tuple-element.21), channel_id=1, source_target_pairs={{0,1},{1,2},{2,3},{3,4},{4,5},{5,6},{6,7},{7,8},{8,9},{9,10},{10,1... | collective-permute-start | bytes 61448 | tf_op jit(solution)/shard_map/ppermute | solution.py:302
  34.4 14.9 %copy-start.6 = (f32[1,64,1024]{2,1,0:T(8,128)S(1)}, f32[1,64,1024]{2,1,0:T(8,128)}, u32[]{:S(2)}) copy-start(f32[1,64,1024]{2,1,0:T(8,128)} %factor_ref.3) | copy-start | bytes 786436
  34.5 6.1 %collective-permute-start.2 = (f32[5,8,128]{2,1,0:T(8,128)S(1)}, f32[5,8,128]{2,1,0:T(8,128)S(1)}, u32[]{:S(2)}, u32[]{:S(2)}) collective-permute-start(f32[5,8,128]{2,1,0:T(8,128)S(1)} %get-tuple-element.22), channel_id=1, source_target_pairs={{1,0},{2,1},{3,2},{4,3},{5,4},{6,5},{7,6},{8,7},{9,8},{10,9},{11,1... | collective-permute-start | bytes 61448 | tf_op jit(solution)/shard_map/ppermute | solution.py:303
